TPU v7x, 32 devices: a whole 2x2x4 slice. The times are simulated.
32 devices in a mesh: grp: 2 (over y), dp: 16 (over z, x, core).
Axes of the slice: x: 2, y: 2, z: 4, core: 2. Of those that a mesh axis runs over, the one named last changes fastest.
Arguments:
- params: float32 [1900544], P(('grp', 'dp')), parts along dimension 0, may hold values from -0.3 to 0.3
- momentum: float32 [1900544], P(('grp', 'dp')), parts along dimension 0, may hold values from -6 to 6
- noise_draws: float32 [2, 950272], P('grp', 'dp'), parts along dimension 0, may hold values from -6 to 6
- images: float32 [16384, 448], P(('grp', 'dp')), parts along dimension 0, may hold values from -6 to 6
- labels: int32 [16384], P(('grp', 'dp')), parts along dimension 0, may hold values from 0 to 9
- indices: int32 [2, 4096], P('grp', 'dp'), parts along dimension 0, may hold values from 0 to 511
Outputs:
- params_out: float32 [1900544], P(('grp', 'dp')), parts along dimension 0
- momentum_out: float32 [1900544], P(('grp', 'dp')), parts along dimension 0
- losses: float32 [2], P('grp'), parts along dimension 0
There are 2 independent parts, one for each index of `grp`. A program takes and returns all parts, laid end to end along the dimension named above; each array names one. Nothing has to cross between parts.
All inputs are finite; a program needn't handle non-finite values.
Results may differ from a plain program's by a relative error of at most 0.0003.
Values sent between devices are 32-bit elements; how exact they have to be, the bound alone decides.
A program may use at most 64 MiB of HBM per device.

v0:
```python
import math

import jax
import jax.numpy as jnp
from jax import lax
from jax.sharding import PartitionSpec as P

DIN = 448
H = 2048
OUT = 10


step_size = 0.02
friction = 15.0


def unpack(flat_vec):
    in_end = DIN * H
    w_in = flat_vec[:in_end].reshape(DIN, H)
    b_in = flat_vec[in_end : in_end + H]
    hid_end = in_end + H
    w_out = flat_vec[hid_end : hid_end + H * OUT].reshape(H, OUT)
    b_out = flat_vec[hid_end + H * OUT : hid_end + H * OUT + OUT]
    return (w_in, b_in, w_out, b_out)


def total_nll(flat_vec, chosen_rows, targets):
    w_in, b_in, w_out, b_out = unpack(flat_vec)
    hidden = jnp.tanh(
        jnp.dot(
            chosen_rows, w_in, precision=lax.Precision.HIGHEST, preferred_element_type=jnp.float32
        )
        + b_in
    )
    logits = (
        jnp.dot(hidden, w_out, precision=lax.Precision.HIGHEST, preferred_element_type=jnp.float32)
        + b_out
    )
    log_norm = jnp.log(jnp.sum(jnp.exp(logits), axis=1))
    classes = lax.broadcasted_iota(jnp.int32, logits.shape, 1)
    picked = jnp.sum(jnp.where(targets[:, None] == classes, logits, 0.0), axis=1)
    return jnp.sum(log_norm - picked)


def prior_precision(flat_index):
    in_end = DIN * H
    hid_end = in_end + H
    out_end = hid_end + H * OUT
    return jnp.where(
        flat_index < in_end,
        float(DIN),
        jnp.where(flat_index < hid_end, 1.0, jnp.where(flat_index < out_end, float(H), 1.0)),
    )


def body(params, momentum, noise_draws, images, labels, indices):
    shard_len = params.shape[0]
    shard_start = lax.axis_index("dp") * shard_len
    precision = prior_precision(shard_start + lax.iota(jnp.int32, shard_len))
    scale_data = images.shape[0] / indices.shape[1]
    row_count = lax.axis_size("dp") * indices.shape[1]
    gathered = lax.all_gather(params, "dp", axis=0, tiled=True)
    picked_rows = indices[0]
    chosen_rows = jnp.take(images, picked_rows, axis=0)
    targets = jnp.take(labels, picked_rows, axis=0)
    nll_part, pullback = jax.vjp(
        lambda weights_flat: total_nll(weights_flat, chosen_rows, targets), gathered
    )
    (local_grad,) = pullback(jnp.ones_like(nll_part))
    losses = [lax.psum(nll_part, "dp") / row_count]
    summed = lax.psum(local_grad, "dp")
    own_grad = lax.dynamic_slice_in_dim(summed, shard_start, shard_len)
    total_force = scale_data * own_grad + precision * params
    momentum = (
        (1.0 - step_size * friction) * momentum
        - step_size * total_force
        + math.sqrt(2.0 * friction * step_size) * noise_draws[0]
    )
    params = params + step_size * momentum
    return (params, momentum, jnp.stack(losses))


def solution(mesh):
    placed = (
        P(("grp", "dp")),
        P(("grp", "dp")),
        P("grp", "dp"),
        P(("grp", "dp"), None),
        P(("grp", "dp")),
        P("grp", "dp"),
    )
    return jax.shard_map(
        body,
        mesh=mesh,
        in_specs=placed,
        out_specs=(P(("grp", "dp")), P(("grp", "dp")), P("grp")),
        check_vma=False,
    )
```

profile of v0, /device:TPU:0, one launch (start us, length us, event | category | flops | bytes accessed | tf_op | source)
XLA Modules:
  0.0 212.2 jit_solution(1588823697586954154)
XLA Ops:
  7.2 0.0 copy-start
  7.2 0.0 all-gather.2.cloned.1.call-start
  7.2 0.7 all-gather.2.cloned.1.call-update
  7.9 0.0 all-reduce.6.cloned.1.call-start
  8.0 1.5 copy.12
  9.5 1.9 gather_fusion
  11.5 1.0 gather_fusion.1
  12.5 48.9 %all-gather.2.cloned.1.call-done = f32[950272]{0:T(1024)} async-done(((f32[59392]{0:T(1024)}), f32[950272]{0:T(1024)}) %all-gather.2.cloned.1.call-update) | async-done | bytes 3801104 | tf_op jit(solution)/shard_map/all_gather | solution.py:62
  61.4 4.1 %slice.31 = f32[917504]{0:T(1024)} slice(f32[950272]{0:T(1024)} %all-gather.2.cloned.1.call-done), slice={[0:917504]} | slice | bytes 7340032 | tf_op jit(solution)/shard_map/jvp()/slice | solution.py:19
  65.5 4.8 %slice.23 = f32[448,2048]{1,0:T(8,128)} reshape(f32[917504]{0:T(1024)} %slice.31) | data formatting | bytes 7340032 | tf_op jit(solution)/shard_map/jvp()/slice | solution.py:19
  70.3 0.0 slice-done
  70.3 1.0 reshape.81
  71.3 0.0 copy-done.1
  71.3 0.0 slice-done.1
  71.3 0.0 slice-start.2
  71.3 5.7 %fusion = f32[256,2048]{1,0:T(8,128)S(1)} fusion(f32[448,2048]{1,0:T(8,128)} %slice.23, f32[2048]{0:T(1024)S(1)} %slice-done.1, f32[256,448]{1,0:T(8,128)S(1)} %gather_fusion.1, pred[256]{0:T(512)(128)(4,1)S(1)} %get-tuple-element.8), kind=kOutput, calls=%fused_computation.4 | convolution fusion | flops 2819211264 | bytes 6234368 | tf_op jit(solution)/shard_map/jvp()/dot_general | solution.py:30
  77.1 1.9 exponential_reduce_fusion
  78.9 0.1 select_reduce_fusion
  79.1 4.5 %fusion.10 = f32[2048,10]{1,0:T(8,128)} fusion(f32[256,2048]{1,0:T(8,128)S(1)} %fusion, f32[256,10]{0,1:T(8,128)S(1)} %get-tuple-element.10, f32[256]{0:T(256)S(1)} %broadcast_divide_fusion, s32[256]{0:T(256)S(1)} %get-tuple-element.7), kind=kOutput, calls=%fused_computation.26 | convolution fusion | flops 62924800 | bytes 2191360 | tf_op jit(solution)/shard_map/transpose(jvp())/dot_general | solution.py:36
  83.6 2.1 fusion.18
  85.7 2.0 reshape.82
  87.7 4.7 %convolution_bitcast_fusion = f32[56,16,8,128]{3,2,1,0:T(8,128)S(1)} fusion(f32[256,2048]{1,0:T(8,128)S(1)} %get-tuple-element.12, f32[256,448]{1,0:T(8,128)} %copy-done.1, pred[256]{0:T(512)(128)(4,1)S(1)} %get-tuple-element.8), kind=kOutput, calls=%fused_computation.6 | convolution fusion | flops 2818686976 | bytes 6226176 | tf_op jit(solution)/shard_map/transpose(jvp())/dot_general | solution.py:30
  92.4 0.8 copy.15
  93.2 2.1 %pad_add_fusion = f32[950272]{0:T(1024)} fusion(f32[917504]{0:T(1024)S(1)} %bitcast.15, f32[2048]{0:T(1024)S(1)} %get-tuple-element.11, f32[20480]{0:T(1024)S(1)} %reshape.82, f32[10]{0:T(128)S(1)} %get-tuple-element.4), kind=kLoop, calls=%fused_computation.2 | loop fusion | flops 2850816 | bytes 7561256 | tf_op jit(solution)/shard_map/transpose(jvp())/add_any | solution.py:19
  95.3 0.0 all-reduce.6.cloned.1.call-update
  95.3 0.9 copy-done.4
  96.2 0.2 broadcast_multiply_fusion
  96.5 0.6 subtract_reduce_fusion
  97.1 32.9 %psum.15 = f32[]{:T(128)} all-reduce(f32[]{:T(128)} %subtract_reduce_fusion), channel_id=1, replica_groups=mesh['grp'=2,'dp'=16] {'dp'}, use_global_device_ids=true, to_apply=%region_6.7 | all-reduce | flops 1 | bytes 8 | tf_op jit(solution)/shard_map/psum | solution.py:70
  130.7 71.6 %all-reduce.6.cloned.1.call-done = f32[950272]{0:T(1024)} async-done(((f32[950272]{0:T(1024)}), f32[950272]{0:T(1024)}) %all-reduce.6.cloned.1.call-update) | async-done | bytes 3801104 | tf_op jit(solution)/shard_map/psum | solution.py:71
  202.3 0.0 copy-done.3
  202.3 1.9 multiply_add_fusion
  (15 shorter events, 0.0 us)
Async XLA Ops:
  7.2 2.4 %copy-start = (s32[512]{0:T(512)S(1)}, s32[512]{0:T(512)}, u32[]{:S(2)}) copy-start(s32[512]{0:T(512)} %param.10) | copy-start | bytes 6148
  7.2 2.3 %copy-start.5 = (s32[1,256]{1,0:T(1,128)S(1)}, s32[1,256]{1,0:T(1,128)}, u32[]{:S(2)}) copy-start(s32[1,256]{1,0:T(1,128)} %param.11) | copy-start | bytes 3076
  7.2 54.2 %all-gather.2.cloned.1.call-start = ((), (), s32[]{:S(2)}) async-start(), calls=%async_computation | async-start | bytes 4038656 | tf_op jit(solution)/shard_map/all_gather | solution.py:62
  7.9 194.4 %all-reduce.6.cloned.1.call-start = ((), (), s32[]{:S(2)}) async-start(), calls=%async_computation.1 | async-start | bytes 7602176 | tf_op jit(solution)/shard_map/psum | solution.py:71
  12.5 58.9 %copy-start.1 = (f32[256,448]{1,0:T(8,128)}, f32[256,448]{1,0:T(8,128)S(1)}, u32[]{:S(2)}) copy-start(f32[256,448]{1,0:T(8,128)S(1)} %gather_fusion.1) | copy-start | bytes 1376260
  65.5 4.8 %slice-start = ((f32[950272]{0:T(1024)}), f32[20480]{0:T(1024)S(1)}, s32[]{:S(2)}) async-start(f32[950272]{0:T(1024)} %all-gather.2.cloned.1.call-done), calls=%async_computation.2 | async-start | bytes 163840 | tf_op jit(solution)/shard_map/jvp()/slice | solution.py:22
  65.5 5.8 %slice-start.1 = ((f32[950272]{0:T(1024)}), f32[2048]{0:T(1024)S(1)}, s32[]{:S(2)}) async-start(f32[950272]{0:T(1024)} %all-gather.2.cloned.1.call-done), calls=%async_computation.3 | async-start | bytes 16384 | tf_op jit(solution)/shard_map/jvp()/slice | solution.py:20
  71.3 5.7 %slice-start.2 = ((f32[950272]{0:T(1024)}), f32[10]{0:T(128)S(1)}, s32[]{:S(2)}) async-start(f32[950272]{0:T(1024)} %all-gather.2.cloned.1.call-done), calls=%async_computation.4 | async-start | bytes 1024 | tf_op jit(solution)/shard_map/jvp()/slice | solution.py:23
  95.3 0.9 copy-start.4
  95.3 107.0 %copy-start.2 = (f32[59392]{0:T(1024)S(1)}, f32[59392]{0:T(1024)}, u32[]{:S(2)}) copy-start(f32[59392]{0:T(1024)} %param.6) | copy-start | bytes 712708
  95.3 107.0 %copy-start.3 = (f32[59392]{0:T(1024)S(1)}, f32[59392]{0:T(1024)}, u32[]{:S(2)}) copy-start(f32[59392]{0:T(1024)} %param.7) | copy-start | bytes 712708
Sparse Core Ops, SparseCore 0:
  10.3 51.0 all-gather.1
  95.5 106.8 all-reduce.5
where the time goes:
time: 213 us; the launch traced here: 212 us
  waiting for transfers between devices  121 us (57%)
  blocking collectives  32.9 us (15%)
  matrix products  18.9 us (9%)
  local copies, waits for them, and re-layouts  18.1 us (8%)
  between operations  16 us (8%)
  other arithmetic  5 us (2%)
    psum x1, waiting for transfers between devices, body(): summed = lax.psum(local_grad, 'dp')  71.6 us
    all_gather x1, waiting for transfers between devices, body(): gathered = lax.all_gather(params, 'dp', axis=0, tiled=True)  48.9 us
    psum x1, blocking collectives, body(): losses = [lax.psum(nll_part, 'dp') / row_count]  32.9 us
    dot_general x2, matrix products, total_nll(): jnp.dot(chosen_rows, w_in, precision=lax.Precision.HIGHEST, preferred_ele...  10.4 us
    slice x2, local copies, waits for them, and re-layouts, unpack(): w_in = flat_vec[:in_end].reshape(DIN, H)  8.86 us
    dot_general x3, matrix products, total_nll(): jnp.dot(hidden, w_out, precision=lax.Precision.HIGHEST, preferred_element...  8.5 us
  transfers between devices with their start and end apart: 2, of which 2 were waited for; matrix products, arithmetic and copies ran while one was open for 2% of the time, Pallas kernels for 0%

commit v1 on v0

--- a/solution.py
+++ b/solution.py
@@ -1,8 +1,11 @@
+import functools
 import math
 
 import jax
 import jax.numpy as jnp
 from jax import lax
+from jax.experimental import pallas as pl
+from jax.experimental.pallas import tpu as pltpu
 from jax.sharding import PartitionSpec as P
 
 DIN = 448
@@ -80,7 +83,409 @@
     return (params, momentum, jnp.stack(losses))
 
 
+PLANE = 4
+DEPTH = 4
+LANES = 128
+BF = jnp.bfloat16
+F32 = jnp.float32
+MESH = pl.DeviceIdType.MESH
+NN = (((1,), (0,)), ((), ()))
+NT = (((1,), (1,)), ((), ()))
+TN = (((0,), (0,)), ((), ()))
+
+
+def halves(a):
+    high = a.astype(BF)
+    return high, (a - high.astype(F32)).astype(BF)
+
+
+def dot(a, b, dims):
+    return lax.dot_general(a, b, dims, preferred_element_type=F32)
+
+
+def dot3(a, b, dims):
+    return dot(a[0], b[0], dims) + (dot(a[0], b[1], dims) + dot(a[1], b[0], dims))
+
+
+def iota(shape, axis):
+    return lax.broadcasted_iota(jnp.int32, shape, axis)
+
+
+def kernel(
+    dims,
+    par, mom, noi, img, lab, idx,
+    par_out, mom_out, loss_out,
+    wsend, wbuf, xall, xh, xl, wh, wl, hid, w2src, w2buf, b2buf, slab, w2t,
+    lsend, lrecv, dsend, drecv, dwz, zrecv, psend, precv, gbuf, w2send, w2recv, tsend, trecv,
+    s_wp, s_wz, r_w, s_x, r_x, s_2, s_b, r_2, r_b, s_l, r_l, s_d, r_d, s_z, r_z, s_p, r_p, s_g, r_g, s_t, r_t,
+):
+    rows, pad, quarter, batch, scale_data, row_count = dims
+    blocks = quarter // LANES
+    colblocks = PLANE * blocks
+    me = lax.axis_index("dp")
+    n = PLANE * DEPTH
+    last = n - 1
+    z = me // PLANE
+    q = me % PLANE
+    x, c = q // 2, q % 2
+    mates = [q, 2 * x + (1 - c), 2 * (1 - x) + c, 2 * (1 - x) + (1 - c)]
+
+    def copy(src, dst, ssem, rsem, to):
+        return pltpu.make_async_remote_copy(
+            src_ref=src, dst_ref=dst, send_sem=ssem, recv_sem=rsem, device_id={"dp": to}, device_id_type=MESH
+        )
+
+    barrier = pltpu.get_barrier_semaphore()
+    for k in range(1, n):
+        pl.semaphore_signal(barrier, inc=1, device_id={"dp": (me + k) % n}, device_id_type=MESH)
+
+    for p in range(PLANE):
+        for j in range(blocks):
+            cols = slice(j * LANES, (j + 1) * LANES)
+            wsend[p, 0:rows, cols] = par[pl.ds(p * blocks + j, rows, stride=colblocks), :]
+        wsend[p, rows:pad, :] = jnp.zeros((pad - rows, quarter), F32)
+    wbuf[pl.ds(pl.multiple_of(me * pad, pad), pad), :] = wsend[q]
+    pool = img.shape[0]
+    onehot = (iota((pool, batch), 0) == idx[...]).astype(BF)
+    target = dot(jnp.broadcast_to(lab[...], (8, pool)).astype(BF), onehot, NN)[0:1, :]
+    ih, il = halves(img[...])
+    wide = n * pad
+    at = iota((DIN, wide), 1)
+    move = ((at % pad < rows) & ((at // pad) * rows + at % pad == iota((DIN, wide), 0))).astype(BF)
+    bias_at = (DIN // rows) * pad + DIN % rows
+    ph = dot(dot(onehot, ih, TN).astype(BF), move, NN)
+    pl_ = dot(dot(onehot, il, TN).astype(BF), move, NN)
+    xall[q] = ph + pl_ + (iota((batch, wide), 1) == bias_at).astype(F32)
+    w2_row = (DIN + 1) * colblocks - last * rows * colblocks
+    per = OUT * blocks
+    for p in range(PLANE):
+        w2src[p] = par[w2_row + p * per : w2_row + (p + 1) * per, :]
+
+    pl.semaphore_wait(barrier, n - 1)
+
+    def wpiece(s):
+        return wbuf.at[pl.ds(pl.multiple_of(s * pad, pad), pad), :]
+
+    plane_w = []
+    for k in (3, 2, 1):
+        o = mates[k]
+        cp = copy(wsend.at[o], wpiece(me), s_wp.at[k], r_w.at[me], z * PLANE + o)
+        cp.start()
+        plane_w.append(cp)
+
+    def zsend(src, s, go, act):
+        for d, ok, to in ((0, z < DEPTH - 1, z + 1), (1, z > 0, z - 1)):
+            if d in go:
+                @pl.when(ok)
+                def _():
+                    getattr(copy(src, wpiece(s), s_wz.at[d, s], r_w.at[s], to * PLANE + q), act)()
+
+    zsend(wsend.at[q], me, (0, 1), "start")
+    b2_row = w2_row + PLANE * per
+
+    @pl.when(me == last)
+    def _():
+        for d in range(n - 1):
+            copy(w2src.at[d % PLANE], w2buf, s_2.at[d], r_2, d).start()
+            copy(par.at[b2_row : b2_row + 8, :], b2buf, s_b.at[d], r_b, d).start()
+        w2buf[...] = w2src[PLANE - 1]
+        b2buf[...] = par[b2_row : b2_row + 8, :]
+
+    x_sends = []
+    for k in (2, 1):
+        cp = copy(xall.at[q], xall.at[q], s_x.at[k], r_x.at[q], z * PLANE + mates[k])
+        cp.start()
+        x_sends.append(cp)
+
+    def w_arrived(s):
+        copy(wsend.at[0], wpiece(s), s_wp.at[0], r_w.at[s], me).wait_recv()
+
+    def x_arrived(k):
+        copy(xall.at[q], xall.at[mates[k]], s_x.at[0], r_x.at[mates[k]], me).wait_recv()
+
+    for k in (1, 2, 3):
+        s = z * PLANE + mates[k]
+        w_arrived(s)
+        zsend(wpiece(s), s, (0, 1), "start")
+
+    def each_far(fn):
+        for t in range(1, DEPTH):
+            for k in range(PLANE):
+                for sign, d in ((-1, 0), (1, 1)):
+                    zs = z + sign * t
+                    s = zs * PLANE + mates[k]
+
+                    @pl.when((zs >= 0) & (zs < DEPTH))
+                    def _(s=s, d=d):
+                        fn(s, d)
+
+    x_arrived(2)
+    cp = copy(xall.at[mates[2]], xall.at[mates[2]], s_x.at[3], r_x.at[mates[2]], z * PLANE + mates[1])
+    cp.start()
+    x_sends.append(cp)
+
+    def forward(s, d):
+        w_arrived(s)
+        zsend(wpiece(s), s, (d,), "start")
+
+    each_far(forward)
+
+    @pl.when(me < last)
+    def _():
+        copy(w2src.at[0], w2buf, s_2.at[0], r_2, me).wait_recv()
+        copy(par.at[b2_row : b2_row + 8, :], b2buf, s_b.at[0], r_b, me).wait_recv()
+
+    slab[...] = jnp.zeros_like(slab)
+    for j in range(blocks):
+        slab[16 * j : 16 * j + OUT, :] = w2buf[OUT * j : OUT * (j + 1), :]
+    sh, sl = halves(slab[...])
+    w2t[...] = jnp.zeros_like(w2t)
+
+    def select(o):
+        at = OUT * iota((LANES, LANES), 1) + o
+        spot = ((at & (LANES - 1)) == iota((LANES, LANES), 0)).astype(BF)
+        at16 = OUT * iota((16, LANES), 1) + o
+        return spot, (at16 // LANES) == iota((16, LANES), 0)
+
+    for o in range(OUT):
+        spot, mask = select(o)
+        r = dot(sh, spot, NN) + dot(sl, spot, NN)
+        for j in range(blocks):
+            w2t[o : o + 1, j * LANES : (j + 1) * LANES] = jnp.sum(
+                jnp.where(mask, r[16 * j : 16 * (j + 1), :], 0.0), axis=0, keepdims=True
+            )
+    w2h = halves(w2t[...])
+    x_arrived(1)
+    x_arrived(3)
+    a, b = halves(wbuf[...])
+    wh[...] = a
+    wl[...] = b
+    l_sends = []
+    for k in (3, 2, 1, 0):
+        o = mates[k]
+        a, b = halves(xall[o])
+        xh[o] = a
+        xl[o] = b
+        h = jnp.tanh(dot3((a, b), (wh[...], wl[...]), NN))
+        hid[o] = h
+        part = dot3(w2h, halves(h), NT)
+        if k == 0:
+            mine = part
+        else:
+            lsend[k] = part
+            cp = copy(lsend.at[k], lrecv.at[q], s_l.at[k], r_l.at[q], z * PLANE + o)
+            cp.start()
+            l_sends.append(cp)
+    logits = mine
+    for k in (1, 2, 3):
+        copy(lsend.at[k], lrecv.at[mates[k]], s_l.at[0], r_l.at[mates[k]], me).wait_recv()
+        logits = logits + lrecv[mates[k]]
+    b2 = jnp.broadcast_to(b2buf[0:1, :], (16, LANES))
+    diag = iota((16, LANES), 0) == iota((16, LANES), 1)
+    logits = logits + jnp.sum(jnp.where(diag, b2, 0.0), axis=1, keepdims=True)
+    cls = iota((16, batch), 0)
+    real = cls < OUT
+    top = jnp.max(jnp.where(real, logits, -3e38), axis=0, keepdims=True)
+    e = jnp.where(real, jnp.exp(jnp.where(real, logits - top, 0.0)), 0.0)
+    total = jnp.sum(e, axis=0, keepdims=True)
+    hit = cls == target.astype(jnp.int32)
+    nll = jnp.log(total) + top - jnp.sum(jnp.where(hit, logits, 0.0), axis=0, keepdims=True)
+    dl = e / total - jnp.where(hit, 1.0, 0.0)
+    dsend[...] = dl
+    drecv[q] = dl
+    d_sends = []
+    for k in (3, 2, 1):
+        cp = copy(dsend, drecv.at[q], s_d.at[k], r_d.at[q], z * PLANE + mates[k])
+        cp.start()
+        d_sends.append(cp)
+    db2 = jnp.sum(dl, axis=1, keepdims=True)
+    db2 = jnp.sum(jnp.where(diag, jnp.broadcast_to(db2, (16, LANES)), 0.0), axis=0, keepdims=True)
+    loss = jnp.sum(nll, axis=1, keepdims=True)
+    tile_row = iota((8, LANES), 0)
+    tile = jnp.where(tile_row == 0, jnp.broadcast_to(db2, (8, LANES)), jnp.broadcast_to(loss, (8, LANES)))
+    tsend[...] = tile
+    trecv[me] = tile
+
+    for k in range(1, PLANE):
+        copy(dsend, drecv.at[mates[k]], s_d.at[0], r_d.at[mates[k]], me).wait_recv()
+    dw2 = jnp.zeros((16, quarter), F32)
+    for p in range(PLANE):
+        h = hid[p]
+        d = halves(drecv[p])
+        dw2 = dw2 + dot3(d, halves(h), NN)
+        hid[p] = dot3(d, w2h, TN) * (1.0 - h * h)
+    dp = [halves(hid[p]) for p in range(PLANE)]
+    z_sends = []
+    chunk = PLANE * pad
+    own = None
+    for k in (3, 2, 1, 0):
+        to = (z + k) % DEPTH
+        cols = pl.ds(pl.multiple_of(to * chunk, chunk), chunk)
+        g = jnp.zeros((chunk, quarter), F32)
+        for p in range(PLANE):
+            g = g + dot3((xh[p, :, cols], xl[p, :, cols]), dp[p], TN)
+        if k == 0:
+            own = g
+        else:
+            dwz[k] = g
+            cp = copy(dwz.at[k], zrecv.at[k], s_z.at[k], r_z.at[k], to * PLANE + q)
+            cp.start()
+            z_sends.append(cp)
+    dwz[0] = own
+    acc = jnp.zeros((16 * blocks, LANES), F32)
+    for o in range(OUT):
+        spot, mask = select(o)
+        g = jnp.concatenate(
+            [
+                jnp.where(mask, jnp.broadcast_to(dw2[o : o + 1, j * LANES : (j + 1) * LANES], (16, LANES)), 0.0)
+                for j in range(blocks)
+            ],
+            axis=0,
+        )
+        gh, gl = halves(g)
+        acc = acc + dot(gh, spot, NT) + dot(gl, spot, NT)
+    slab[...] = acc
+    for j in range(blocks):
+        w2send[OUT * j : OUT * (j + 1), :] = slab[16 * j : 16 * j + OUT, :]
+
+    t_sends = []
+    for k in range(1, n):
+        cp = copy(tsend, trecv.at[me], s_t.at[k], r_t.at[me], (me + k) % n)
+        cp.start()
+        t_sends.append(cp)
+
+    @pl.when(me < last)
+    def _():
+        copy(w2send, w2recv.at[me], s_g, r_g.at[me], last).start()
+
+    @pl.when(me == last)
+    def _():
+        w2recv[last] = w2send[...]
+
+    own = dwz[0]
+    for k in range(1, DEPTH):
+        copy(dwz.at[k], zrecv.at[k], s_z.at[0], r_z.at[k], me).wait_recv()
+        own = own + zrecv[k]
+    for p in range(PLANE):
+        psend[p] = own[p * pad : (p + 1) * pad, :]
+    precv[q] = psend[q]
+    p_sends = []
+    for k in (3, 2, 1):
+        cp = copy(psend.at[mates[k]], precv.at[q], s_p.at[k], r_p.at[q], z * PLANE + mates[k])
+        cp.start()
+        p_sends.append(cp)
+
+    for k in range(1, n):
+        s = (me + k) % n
+        copy(tsend, trecv.at[s], s_t.at[0], r_t.at[s], me).wait_recv()
+    sums = trecv[0]
+    for s in range(1, n):
+        sums = sums + trecv[s]
+    loss_out[0] = sums[1, 0] / row_count
+
+    for k in range(1, PLANE):
+        copy(psend.at[0], precv.at[mates[k]], s_p.at[0], r_p.at[mates[k]], me).wait_recv()
+    for p in range(PLANE):
+        for j in range(blocks):
+            gbuf[pl.ds(p * blocks + j, rows, stride=colblocks), :] = precv[p, 0:rows, j * LANES : (j + 1) * LANES]
+
+    @pl.when(me == last)
+    def _():
+        for s in range(n - 1):
+            copy(w2send, w2recv.at[s], s_g, r_g.at[s], me).wait_recv()
+        for p in range(PLANE):
+            g = w2recv[p]
+            for d in range(1, DEPTH):
+                g = g + w2recv[d * PLANE + p]
+            gbuf[w2_row + p * per : w2_row + (p + 1) * per, :] = g
+        gbuf[b2_row : b2_row + 8, :] = jnp.where(tile_row == 0, sums, 0.0)
+
+    flat_rows = rows * colblocks
+    position = (me * flat_rows + iota((flat_rows, LANES), 0)) * LANES
+    force = scale_data * gbuf[...] + prior_precision(position) * par[...]
+    m = (
+        (1.0 - step_size * friction) * mom[...]
+        - step_size * force
+        + math.sqrt(2.0 * friction * step_size) * noi[...]
+    )
+    mom_out[...] = m
+    par_out[...] = par[...] + step_size * m
+
+    for cp in plane_w + x_sends + l_sends + d_sends + z_sends + t_sends + p_sends:
+        cp.wait_send()
+    for k in range(PLANE):
+        s = z * PLANE + mates[k]
+        zsend(wsend.at[q], s, (0, 1), "wait_send")
+    each_far(lambda s, d: zsend(wsend.at[q], s, (d,), "wait_send"))
+
+    @pl.when(me == last)
+    def _():
+        for d in range(n - 1):
+            copy(w2src.at[d % PLANE], w2buf, s_2.at[d], r_2, d).wait_send()
+            copy(par.at[b2_row : b2_row + 8, :], b2buf, s_b.at[d], r_b, d).wait_send()
+
+    @pl.when(me < last)
+    def _():
+        copy(w2send, w2recv.at[me], s_g, r_g.at[me], last).wait_send()
+
+
+def fused_body(params, momentum, noise_draws, images, labels, indices):
+    n = PLANE * DEPTH
+    shard = params.shape[0]
+    rows = shard // H
+    pad = -(-rows // 8) * 8
+    quarter = H // PLANE
+    blocks = quarter // LANES
+    per = OUT * blocks
+    batch = indices.shape[1]
+    flat = (shard // LANES, LANES)
+    dims = (rows, pad, quarter, batch, images.shape[0] / batch, n * batch)
+    wide = n * pad
+    chunk = PLANE * pad
+    sem = lambda *s: pltpu.SemaphoreType.DMA(s)
+    one = pltpu.SemaphoreType.DMA
+    vm = lambda *s: pltpu.VMEM(s, F32)
+    scratch = [
+        vm(PLANE, pad, quarter), vm(wide, quarter), vm(PLANE, batch, wide),
+        pltpu.VMEM((PLANE, batch, wide), BF), pltpu.VMEM((PLANE, batch, wide), BF),
+        pltpu.VMEM((wide, quarter), BF), pltpu.VMEM((wide, quarter), BF),
+        vm(PLANE, batch, quarter), vm(PLANE, per, LANES), vm(per, LANES), vm(8, LANES),
+        vm(16 * blocks, LANES), vm(16, quarter),
+        vm(PLANE, 16, batch), vm(PLANE, 16, batch), vm(16, batch), vm(PLANE, 16, batch),
+        vm(DEPTH, chunk, quarter), vm(DEPTH, chunk, quarter),
+        vm(PLANE, pad, quarter), vm(PLANE, pad, quarter), vm(*flat),
+        vm(per, LANES), vm(n, per, LANES), vm(8, LANES), vm(n, 8, LANES),
+        sem(4), sem(2, n), sem(n), sem(4), sem(4), sem(n), sem(n), one, one,
+        sem(4), sem(4), sem(4), sem(4), sem(4), sem(4), sem(4), sem(4), one, sem(n), sem(n), sem(n),
+    ]
+    vmem = pl.BlockSpec(memory_space=pltpu.VMEM)
+    p, m, loss = pl.pallas_call(
+        functools.partial(kernel, dims),
+        out_shape=(
+            jax.ShapeDtypeStruct(flat, F32),
+            jax.ShapeDtypeStruct(flat, F32),
+            jax.ShapeDtypeStruct((1,), F32),
+        ),
+        in_specs=[vmem] * 6,
+        out_specs=(vmem, vmem, pl.BlockSpec(memory_space=pltpu.SMEM)),
+        scratch_shapes=scratch,
+        compiler_params=pltpu.CompilerParams(
+            collective_id=0, has_side_effects=True, vmem_limit_bytes=56 * 2**20
+        ),
+    )(
+        params.reshape(flat),
+        momentum.reshape(flat),
+        noise_draws.reshape(flat),
+        images,
+        labels.reshape(1, -1),
+        indices,
+    )
+    return (p.reshape(-1), m.reshape(-1), loss)
+
+
 def solution(mesh):
+    fits = mesh.shape["dp"] == PLANE * DEPTH
+    step = fused_body if fits else body
     placed = (
         P(("grp", "dp")),
         P(("grp", "dp")),
@@ -90,7 +495,7 @@
         P("grp", "dp"),
     )
     return jax.shard_map(
-        body,
+        step,
         mesh=mesh,
         in_specs=placed,
         out_specs=(P(("grp", "dp")), P(("grp", "dp")), P("grp")),

time: 213 us -> 80.5 us (0.38)
  waiting for transfers between devices: 121 us -> 0 us
  Pallas kernels: 0 us -> 73 us
  blocking collectives: 32.9 us -> 0 us
  matrix products: 18.9 us -> 0 us
  between operations: 16 us -> 2.38 us
  local copies, waits for them, and re-layouts: 18.1 us -> 4.89 us
  other arithmetic: 5 us -> 0 us
    pallas_call x0 -> x1, Pallas kernels: none -> 73 us  [fused_body(): pl.pallas_call(functools.partial(kernel, dims), out_shape=(jax.ShapeDtype...]
    psum x1 -> x0, waiting for transfers between devices: 71.6 us -> none  [body(): summed = lax.psum(local_grad, 'dp')]
    all_gather x1 -> x0, waiting for transfers between devices: 48.9 us -> none  [body(): gathered = lax.all_gather(params, 'dp', axis=0, tiled=True)]
    psum x1 -> x0, blocking collectives: 32.9 us -> none  [body(): losses = [lax.psum(nll_part, 'dp') / row_count]]
    dot_general x5 -> x0, matrix products: 18.9 us -> none  [the longest x2 10.4 us: total_nll(): jnp.dot(chosen_rows, w_in, precision=lax.Precision.HIGHEST, preferred_ele...]
    slice x8 -> x0, local copies, waits for them, and re-layouts: 8.87 us -> none  [the longest x2 8.86 us: unpack(): w_in = flat_vec[:in_end].reshape(DIN, H)]
    reshape x2 -> x0, local copies, waits for them, and re-layouts: 3.04 us -> none  [unpack(): w_out = flat_vec[hid_end:hid_end + H * OUT].reshape(H, OUT)]
    gather x2 -> x0, local copies, waits for them, and re-layouts: 2.92 us -> none  [the longest x1 1.95 us: body(): targets = jnp.take(labels, picked_rows, axis=0)]
  transfers between devices with their start and end apart: 2 -> 0, of which waited for: 2 -> 0; matrix products, arithmetic and copies ran while one was open for 2% -> 0% of each run, Pallas kernels for 0% -> 0%
where the time goes in v1:
time: 80.5 us; the launch traced here: 80.3 us
  Pallas kernels  73 us (91%)
  local copies, waits for them, and re-layouts  4.89 us (6%)
  between operations  2.38 us (3%)
    pallas_call x1, Pallas kernels, fused_body(): pl.pallas_call(functools.partial(kernel, dims), out_shape=(jax.ShapeDtype...  73 us
    unnamed x5, local copies, waits for them, and re-layouts  4.89 us

profile of v1, /device:TPU:0, one launch (start us, length us, event | category | flops | bytes accessed | tf_op | source)
XLA Modules:
  0.0 80.3 jit_solution(5671895836834700245)
XLA Ops:
  0.6 2.5 %copy.9.img = f32[512,448]{1,0:T(8,128)} copy(f32[512,448]{0,1:T(8,128)} %param.9) | data formatting | bytes 1835008 | tf_op args[3]
  3.1 73.0 %shard_map.85 = (f32[464,128]{1,0:T(8,128)}, f32[464,128]{1,0:T(8,128)}, f32[1]{0:T(128)}) custom-call(f32[464,128]{1,0:T(8,128)} %bitcast.8, f32[464,128]{1,0:T(8,128)} %bitcast.9, f32[464,128]{1,0:T(8,128)} %bitcast.10, f32[512,448]{1,0:T(8,128)} %copy.9.img, s32[1,512]{1,0:T(1,128)} %bitcast.11, s32[1,256]{1,0:T(1,128)} %idx.1), custom_call_target="tpu_custom_call" | custom-call | tf_op jit(solution)/shard_map/pallas_call | solution.py:462
  76.1 0.0 copy-start
  76.1 1.7 %copy.13 = f32[59392]{0:T(1024)} copy(f32[59392]{0:T(1024)} %bitcast.7) | data formatting | bytes 475136
  77.8 0.0 copy-done
  77.8 0.7 copy.14
Async XLA Ops:
  76.1 1.7 %copy-start = (f32[464,128]{1,0:T(8,128)S(1)}, f32[464,128]{1,0:T(8,128)}, u32[]{:S(2)}) copy-start(f32[464,128]{1,0:T(8,128)} %get-tuple-element.7) | copy-start | bytes 712708

commit v2 on v1

--- a/solution.py
+++ b/solution.py
@@ -113,13 +113,13 @@
 
 def kernel(
     dims,
-    par, mom, noi, img, lab, idx,
-    par_out, mom_out, loss_out,
-    wsend, wbuf, xall, xh, xl, wh, wl, hid, w2src, w2buf, b2buf, slab, w2t,
-    lsend, lrecv, dsend, drecv, dwz, zrecv, psend, precv, gbuf, w2send, w2recv, tsend, trecv,
+    par, img, lab, idx,
+    gbuf, loss_out,
+    wsend, wbuf, xall, xh, xl, hid, w2src, w2buf, b2buf, slab, w2t,
+    lsend, lrecv, dsend, drecv, dwz, zrecv, psend, precv, w2send, w2recv, tsend, trecv,
     s_wp, s_wz, r_w, s_x, r_x, s_2, s_b, r_2, r_b, s_l, r_l, s_d, r_d, s_z, r_z, s_p, r_p, s_g, r_g, s_t, r_t,
 ):
-    rows, pad, quarter, batch, scale_data, row_count = dims
+    rows, pad, quarter, batch, row_count = dims
     blocks = quarter // LANES
     colblocks = PLANE * blocks
     me = lax.axis_index("dp")
@@ -145,7 +145,7 @@
             wsend[p, 0:rows, cols] = par[pl.ds(p * blocks + j, rows, stride=colblocks), :]
         wsend[p, rows:pad, :] = jnp.zeros((pad - rows, quarter), F32)
     wbuf[pl.ds(pl.multiple_of(me * pad, pad), pad), :] = wsend[q]
-    pool = img.shape[0]
+    pool = img.shape[1]
     onehot = (iota((pool, batch), 0) == idx[...]).astype(BF)
     target = dot(jnp.broadcast_to(lab[...], (8, pool)).astype(BF), onehot, NN)[0:1, :]
     ih, il = halves(img[...])
@@ -153,8 +153,8 @@
     at = iota((DIN, wide), 1)
     move = ((at % pad < rows) & ((at // pad) * rows + at % pad == iota((DIN, wide), 0))).astype(BF)
     bias_at = (DIN // rows) * pad + DIN % rows
-    ph = dot(dot(onehot, ih, TN).astype(BF), move, NN)
-    pl_ = dot(dot(onehot, il, TN).astype(BF), move, NN)
+    ph = dot(dot(ih, onehot, NN).astype(BF), move, TN)
+    pl_ = dot(dot(il, onehot, NN).astype(BF), move, TN)
     xall[q] = ph + pl_ + (iota((batch, wide), 1) == bias_at).astype(F32)
     w2_row = (DIN + 1) * colblocks - last * rows * colblocks
     per = OUT * blocks
@@ -208,27 +208,35 @@
         w_arrived(s)
         zsend(wpiece(s), s, (0, 1), "start")
 
-    def each_far(fn):
-        for t in range(1, DEPTH):
-            for k in range(PLANE):
-                for sign, d in ((-1, 0), (1, 1)):
-                    zs = z + sign * t
-                    s = zs * PLANE + mates[k]
-
-                    @pl.when((zs >= 0) & (zs < DEPTH))
-                    def _(s=s, d=d):
-                        fn(s, d)
-
+    def far(t, fn):
+        for sign, d in ((-1, 0), (1, 1)):
+            zs = z + sign * t
+
+            @pl.when((zs >= 0) & (zs < DEPTH))
+            def _(zs=zs, d=d):
+                fn(zs, d)
+
+    def forward(zs, d):
+        for k in range(PLANE):
+            s = zs * PLANE + mates[k]
+            w_arrived(s)
+            zsend(wpiece(s), s, (d,), "start")
+
+    chunk = PLANE * pad
+
+    def product(zs, first=False):
+        at = pl.ds(pl.multiple_of(zs * chunk, chunk), chunk)
+        w = halves(wbuf[at, :])
+        for p in range(PLANE):
+            part = dot3((xh[p, :, at], xl[p, :, at]), w, NN)
+            hid[p] = part if first else hid[p] + part
+
+    far(1, forward)
     x_arrived(2)
     cp = copy(xall.at[mates[2]], xall.at[mates[2]], s_x.at[3], r_x.at[mates[2]], z * PLANE + mates[1])
     cp.start()
     x_sends.append(cp)
-
-    def forward(s, d):
-        w_arrived(s)
-        zsend(wpiece(s), s, (d,), "start")
-
-    each_far(forward)
+    far(2, forward)
 
     @pl.when(me < last)
     def _():
@@ -257,16 +265,19 @@
     w2h = halves(w2t[...])
     x_arrived(1)
     x_arrived(3)
-    a, b = halves(wbuf[...])
-    wh[...] = a
-    wl[...] = b
+    for p in range(PLANE):
+        a, b = halves(xall[p])
+        xh[p] = a
+        xl[p] = b
+    product(z, True)
+    far(1, lambda zs, d: product(zs))
+    far(2, lambda zs, d: product(zs))
+    far(3, forward)
+    far(3, lambda zs, d: product(zs))
     l_sends = []
     for k in (3, 2, 1, 0):
         o = mates[k]
-        a, b = halves(xall[o])
-        xh[o] = a
-        xl[o] = b
-        h = jnp.tanh(dot3((a, b), (wh[...], wl[...]), NN))
+        h = jnp.tanh(hid[o])
         hid[o] = h
         part = dot3(w2h, halves(h), NT)
         if k == 0:
@@ -315,23 +326,41 @@
         dw2 = dw2 + dot3(d, halves(h), NN)
         hid[p] = dot3(d, w2h, TN) * (1.0 - h * h)
     dp = [halves(hid[p]) for p in range(PLANE)]
-    z_sends = []
-    chunk = PLANE * pad
-    own = None
-    for k in (3, 2, 1, 0):
-        to = (z + k) % DEPTH
-        cols = pl.ds(pl.multiple_of(to * chunk, chunk), chunk)
+
+    def hop(d, p, right, act):
+        side = 0 if right else 1
+        piece = pl.ds(p * pad, pad)
+        getattr(
+            copy(dwz.at[d, piece], zrecv.at[side, d, piece], s_z.at[d, p], r_z.at[side, d, p],
+                 me + (PLANE if right else -PLANE)),
+            act,
+        )()
+
+    half = z // (DEPTH // 2)
+    for base in (DEPTH - 1, 0, 2, 1):
+        d = base + half * (DEPTH - 1 - 2 * base)
+        cols = pl.ds(pl.multiple_of(d * chunk, chunk), chunk)
         g = jnp.zeros((chunk, quarter), F32)
         for p in range(PLANE):
             g = g + dot3((xh[p, :, cols], xl[p, :, cols]), dp[p], TN)
-        if k == 0:
-            own = g
-        else:
-            dwz[k] = g
-            cp = copy(dwz.at[k], zrecv.at[k], s_z.at[k], r_z.at[k], to * PLANE + q)
-            cp.start()
-            z_sends.append(cp)
-    dwz[0] = own
+        dwz[d] = g
+
+        @pl.when((z == 0) & (d > 0))
+        def _(d=d):
+            for p in range(PLANE):
+                hop(d, p, True, "start")
+
+        @pl.when((z == DEPTH - 1) & (d < DEPTH - 1))
+        def _(d=d):
+            for p in range(PLANE):
+                hop(d, p, False, "start")
+
+    def add_arrived(d, p, right):
+        side = 0 if right else 1
+        piece = pl.ds(p * pad, pad)
+        copy(dwz.at[0, piece], zrecv.at[side, d, piece], s_z.at[0, 0], r_z.at[side, d, p], me).wait_recv()
+        dwz[d, piece, :] = dwz[d, piece, :] + zrecv[side, d, piece, :]
+
     acc = jnp.zeros((16 * blocks, LANES), F32)
     for o in range(OUT):
         spot, mask = select(o)
@@ -362,18 +391,38 @@
     def _():
         w2recv[last] = w2send[...]
 
-    own = dwz[0]
-    for k in range(1, DEPTH):
-        copy(dwz.at[k], zrecv.at[k], s_z.at[0], r_z.at[k], me).wait_recv()
-        own = own + zrecv[k]
-    for p in range(PLANE):
-        psend[p] = own[p * pad : (p + 1) * pad, :]
-    precv[q] = psend[q]
-    p_sends = []
-    for k in (3, 2, 1):
-        cp = copy(psend.at[mates[k]], precv.at[q], s_p.at[k], r_p.at[q], z * PLANE + mates[k])
-        cp.start()
-        p_sends.append(cp)
+    for dr in range(DEPTH - 1, 0, -1):
+        dl_ = DEPTH - 1 - dr
+        for p in range(PLANE):
+            @pl.when((z > 0) & (z < dr))
+            def _(p=p):
+                add_arrived(dr, p, True)
+                hop(dr, p, True, "start")
+
+            @pl.when((z < DEPTH - 1) & (z > dl_))
+            def _(p=p):
+                add_arrived(dl_, p, False)
+                hop(dl_, p, False, "start")
+
+    for p in range(PLANE):
+        @pl.when(z > 0)
+        def _(p=p):
+            add_arrived(z, p, True)
+
+        @pl.when(z < DEPTH - 1)
+        def _(p=p):
+            add_arrived(z, p, False)
+
+        piece = dwz[z, p * pad : (p + 1) * pad, :]
+
+        @pl.when(p == q)
+        def _(p=p, piece=piece):
+            precv[p] = piece
+
+        @pl.when(p != q)
+        def _(p=p, piece=piece):
+            psend[p] = piece
+            copy(psend.at[p], precv.at[q], s_p.at[p], r_p.at[q], z * PLANE + p).start()
 
     for k in range(1, n):
         s = (me + k) % n
@@ -400,23 +449,32 @@
             gbuf[w2_row + p * per : w2_row + (p + 1) * per, :] = g
         gbuf[b2_row : b2_row + 8, :] = jnp.where(tile_row == 0, sums, 0.0)
 
-    flat_rows = rows * colblocks
-    position = (me * flat_rows + iota((flat_rows, LANES), 0)) * LANES
-    force = scale_data * gbuf[...] + prior_precision(position) * par[...]
-    m = (
-        (1.0 - step_size * friction) * mom[...]
-        - step_size * force
-        + math.sqrt(2.0 * friction * step_size) * noi[...]
-    )
-    mom_out[...] = m
-    par_out[...] = par[...] + step_size * m
-
-    for cp in plane_w + x_sends + l_sends + d_sends + z_sends + t_sends + p_sends:
+    for cp in plane_w + x_sends + l_sends + d_sends + t_sends:
         cp.wait_send()
     for k in range(PLANE):
         s = z * PLANE + mates[k]
         zsend(wsend.at[q], s, (0, 1), "wait_send")
-    each_far(lambda s, d: zsend(wsend.at[q], s, (d,), "wait_send"))
+
+    def sent(zs, d):
+        for k in range(PLANE):
+            zsend(wsend.at[q], zs * PLANE + mates[k], (d,), "wait_send")
+
+    for t in range(1, DEPTH):
+        far(t, sent)
+
+    for p in range(PLANE):
+        for d in range(DEPTH):
+            @pl.when(z < d)
+            def _(p=p, d=d):
+                hop(d, p, True, "wait_send")
+
+            @pl.when(z > d)
+            def _(p=p, d=d):
+                hop(d, p, False, "wait_send")
+
+        @pl.when(p != q)
+        def _(p=p):
+            copy(psend.at[p], precv.at[q], s_p.at[p], r_p.at[q], z * PLANE + p).wait_send()
 
     @pl.when(me == last)
     def _():
@@ -439,7 +497,7 @@
     per = OUT * blocks
     batch = indices.shape[1]
     flat = (shard // LANES, LANES)
-    dims = (rows, pad, quarter, batch, images.shape[0] / batch, n * batch)
+    dims = (rows, pad, quarter, batch, n * batch)
     wide = n * pad
     chunk = PLANE * pad
     sem = lambda *s: pltpu.SemaphoreType.DMA(s)
@@ -448,39 +506,43 @@
     scratch = [
         vm(PLANE, pad, quarter), vm(wide, quarter), vm(PLANE, batch, wide),
         pltpu.VMEM((PLANE, batch, wide), BF), pltpu.VMEM((PLANE, batch, wide), BF),
-        pltpu.VMEM((wide, quarter), BF), pltpu.VMEM((wide, quarter), BF),
         vm(PLANE, batch, quarter), vm(PLANE, per, LANES), vm(per, LANES), vm(8, LANES),
         vm(16 * blocks, LANES), vm(16, quarter),
         vm(PLANE, 16, batch), vm(PLANE, 16, batch), vm(16, batch), vm(PLANE, 16, batch),
-        vm(DEPTH, chunk, quarter), vm(DEPTH, chunk, quarter),
-        vm(PLANE, pad, quarter), vm(PLANE, pad, quarter), vm(*flat),
+        vm(DEPTH, chunk, quarter), vm(2, DEPTH, chunk, quarter),
+        vm(PLANE, pad, quarter), vm(PLANE, pad, quarter),
         vm(per, LANES), vm(n, per, LANES), vm(8, LANES), vm(n, 8, LANES),
         sem(4), sem(2, n), sem(n), sem(4), sem(4), sem(n), sem(n), one, one,
-        sem(4), sem(4), sem(4), sem(4), sem(4), sem(4), sem(4), sem(4), one, sem(n), sem(n), sem(n),
+        sem(4), sem(4), sem(4), sem(4), sem(4, 4), sem(2, 4, 4), sem(4), sem(4), one, sem(n), sem(n), sem(n),
     ]
     vmem = pl.BlockSpec(memory_space=pltpu.VMEM)
-    p, m, loss = pl.pallas_call(
+    grad, loss = pl.pallas_call(
         functools.partial(kernel, dims),
         out_shape=(
             jax.ShapeDtypeStruct(flat, F32),
-            jax.ShapeDtypeStruct(flat, F32),
             jax.ShapeDtypeStruct((1,), F32),
         ),
-        in_specs=[vmem] * 6,
-        out_specs=(vmem, vmem, pl.BlockSpec(memory_space=pltpu.SMEM)),
+        in_specs=[vmem] * 4,
+        out_specs=(vmem, pl.BlockSpec(memory_space=pltpu.SMEM)),
         scratch_shapes=scratch,
         compiler_params=pltpu.CompilerParams(
             collective_id=0, has_side_effects=True, vmem_limit_bytes=56 * 2**20
         ),
     )(
         params.reshape(flat),
-        momentum.reshape(flat),
-        noise_draws.reshape(flat),
-        images,
+        images.T,
         labels.reshape(1, -1),
         indices,
     )
-    return (p.reshape(-1), m.reshape(-1), loss)
+    position = lax.axis_index("dp") * shard + iota(flat, 0) * LANES
+    params = params.reshape(flat)
+    force = images.shape[0] / batch * grad + prior_precision(position) * params
+    momentum = (
+        (1.0 - step_size * friction) * momentum.reshape(flat)
+        - step_size * force
+        + math.sqrt(2.0 * friction * step_size) * noise_draws.reshape(flat)
+    )
+    return ((params + step_size * momentum).reshape(-1), momentum.reshape(-1), loss)
 
 
 def solution(mesh):

time: 80.5 us -> 86.2 us (1.071)
  Pallas kernels: 73 us -> 79.7 us
  local copies, waits for them, and re-layouts: 4.89 us -> 0.01 us
  other arithmetic: 0 us -> 3.18 us
    pallas_call x1, Pallas kernels: 73 us -> 79.7 us  [fused_body(): pl.pallas_call(functools.partial(kernel, dims), out_shape=(jax.ShapeDtype...]
    unnamed x5 -> x4, local copies, waits for them, and re-layouts: 4.89 us -> 0.01 us
    reshape x0 -> x1, other arithmetic: none -> 1.97 us  [fused_body(): (params + step_size * momentum).reshape(-1)]
    mul x0 -> x1, other arithmetic: none -> 1.19 us  [fused_body(): math.sqrt(2.0 * friction * step_size) * noise_draws.reshape(flat)]
where the time goes in v2:
time: 86.2 us; the launch traced here: 85.4 us
  Pallas kernels  79.7 us (92%)
  other arithmetic  3.18 us (4%)
  between operations  2.51 us (3%)
    pallas_call x1, Pallas kernels, fused_body(): pl.pallas_call(functools.partial(kernel, dims), out_shape=(jax.ShapeDtype...  79.7 us
    reshape x1, other arithmetic, fused_body(): (params + step_size * momentum).reshape(-1)  1.97 us

profile of v2, /device:TPU:0, one launch (start us, length us, event | category | flops | bytes accessed | tf_op | source)
XLA Modules:
  0.0 85.4 jit_solution(7858746426282378292)
XLA Ops:
  0.7 1.2 %broadcast_multiply_fusion = f32[1,59392]{1,0:T(1,128)S(1)} fusion(f32[1,59392]{1,0:T(1,128)} %param.8), kind=kLoop, calls=%fused_computation.3 | loop fusion | flops 59392 | bytes 475136 | tf_op jit(solution)/shard_map/mul | solution.py:543
  1.9 0.0 copy-start
  1.9 0.0 copy-start.1
  1.9 79.7 %shard_map.85 = (f32[464,128]{1,0:T(8,128)}, f32[1]{0:T(128)}) custom-call(f32[464,128]{1,0:T(8,128)} %bitcast.16, f32[448,512]{1,0:T(8,128)} %bitcast.17, s32[1,512]{1,0:T(1,128)} %bitcast.19, s32[1,256]{1,0:T(1,128)} %idx.1), custom_call_target="tpu_custom_call" | custom-call | tf_op jit(solution)/shard_map/pallas_call | solution.py:519
  81.6 0.0 copy-done
  81.6 0.0 copy-done.1
  81.6 2.0 %add_bitcast_fusion = (f32[59392]{0:T(1024)}, f32[464,128]{1,0:T(8,128)}) fusion(f32[59392]{0:T(1024)S(1)} %copy-done, f32[464,128]{1,0:T(8,128)S(1)} %bitcast.15, f32[464]{0:T(512)S(1)} %fusion.4, pred[464]{0:T(512)(128)(4,1)S(1)} %get-tuple-element.9, pred[464]{0:T(512)(128)(4,1)S(1)} %get-tuple-element.10, f32[464,128]{1,0:T(8,128)} %get-tuple-element.5, ...), kind=kLoop, calls=%fused_computation.2 | loop fusion | flops 653312 | bytes 1428192 | tf_op jit(solution)/shard_map/reshape | solution.py:545
  (2 shorter events, 0.0 us)
Async XLA Ops:
  1.9 79.7 %copy-start = (f32[59392]{0:T(1024)S(1)}, f32[59392]{0:T(1024)}, u32[]{:S(2)}) copy-start(f32[59392]{0:T(1024)} %param.6) | copy-start | bytes 712708
  1.9 79.7 %copy-start.1 = (f32[59392]{0:T(1024)S(1)}, f32[59392]{0:T(1024)}, u32[]{:S(2)}) copy-start(f32[59392]{0:T(1024)} %param.7) | copy-start | bytes 712708

commit v3 on v2

--- a/solution.py
+++ b/solution.py
@@ -115,7 +115,7 @@
     dims,
     par, img, lab, idx,
     gbuf, loss_out,
-    wsend, wbuf, xall, xh, xl, hid, w2src, w2buf, b2buf, slab, w2t,
+    wsend, wbuf, xall, xh, xl, hid, dh, dlow, w2src, w2buf, b2buf, slab, w2t,
     lsend, lrecv, dsend, drecv, dwz, zrecv, psend, precv, w2send, w2recv, tsend, trecv,
     s_wp, s_wz, r_w, s_x, r_x, s_2, s_b, r_2, r_b, s_l, r_l, s_d, r_d, s_z, r_z, s_p, r_p, s_g, r_g, s_t, r_t,
 ):
@@ -145,6 +145,41 @@
             wsend[p, 0:rows, cols] = par[pl.ds(p * blocks + j, rows, stride=colblocks), :]
         wsend[p, rows:pad, :] = jnp.zeros((pad - rows, quarter), F32)
     wbuf[pl.ds(pl.multiple_of(me * pad, pad), pad), :] = wsend[q]
+    w2_row = (DIN + 1) * colblocks - last * rows * colblocks
+    per = OUT * blocks
+    for p in range(PLANE):
+        w2src[p] = par[w2_row + p * per : w2_row + (p + 1) * per, :]
+
+    pl.semaphore_wait(barrier, n - 1)
+
+    def wpiece(s):
+        return wbuf.at[pl.ds(pl.multiple_of(s * pad, pad), pad), :]
+
+    plane_w = []
+    for k in (3, 2, 1):
+        o = mates[k]
+        cp = copy(wsend.at[o], wpiece(me), s_wp.at[k], r_w.at[me], z * PLANE + o)
+        cp.start()
+        plane_w.append(cp)
+
+    def zsend(src, s, go, act):
+        for d, ok, to in ((0, z < DEPTH - 1, z + 1), (1, z > 0, z - 1)):
+            if d in go:
+                @pl.when(ok)
+                def _():
+                    getattr(copy(src, wpiece(s), s_wz.at[d, s], r_w.at[s], to * PLANE + q), act)()
+
+    zsend(wsend.at[q], me, (0, 1), "start")
+    b2_row = w2_row + PLANE * per
+
+    @pl.when(me == last)
+    def _():
+        for d in range(n - 1):
+            copy(w2src.at[d % PLANE], w2buf, s_2.at[d], r_2, d).start()
+            copy(par.at[b2_row : b2_row + 8, :], b2buf, s_b.at[d], r_b, d).start()
+        w2buf[...] = w2src[PLANE - 1]
+        b2buf[...] = par[b2_row : b2_row + 8, :]
+
     pool = img.shape[1]
     onehot = (iota((pool, batch), 0) == idx[...]).astype(BF)
     target = dot(jnp.broadcast_to(lab[...], (8, pool)).astype(BF), onehot, NN)[0:1, :]
@@ -156,41 +191,6 @@
     ph = dot(dot(ih, onehot, NN).astype(BF), move, TN)
     pl_ = dot(dot(il, onehot, NN).astype(BF), move, TN)
     xall[q] = ph + pl_ + (iota((batch, wide), 1) == bias_at).astype(F32)
-    w2_row = (DIN + 1) * colblocks - last * rows * colblocks
-    per = OUT * blocks
-    for p in range(PLANE):
-        w2src[p] = par[w2_row + p * per : w2_row + (p + 1) * per, :]
-
-    pl.semaphore_wait(barrier, n - 1)
-
-    def wpiece(s):
-        return wbuf.at[pl.ds(pl.multiple_of(s * pad, pad), pad), :]
-
-    plane_w = []
-    for k in (3, 2, 1):
-        o = mates[k]
-        cp = copy(wsend.at[o], wpiece(me), s_wp.at[k], r_w.at[me], z * PLANE + o)
-        cp.start()
-        plane_w.append(cp)
-
-    def zsend(src, s, go, act):
-        for d, ok, to in ((0, z < DEPTH - 1, z + 1), (1, z > 0, z - 1)):
-            if d in go:
-                @pl.when(ok)
-                def _():
-                    getattr(copy(src, wpiece(s), s_wz.at[d, s], r_w.at[s], to * PLANE + q), act)()
-
-    zsend(wsend.at[q], me, (0, 1), "start")
-    b2_row = w2_row + PLANE * per
-
-    @pl.when(me == last)
-    def _():
-        for d in range(n - 1):
-            copy(w2src.at[d % PLANE], w2buf, s_2.at[d], r_2, d).start()
-            copy(par.at[b2_row : b2_row + 8, :], b2buf, s_b.at[d], r_b, d).start()
-        w2buf[...] = w2src[PLANE - 1]
-        b2buf[...] = par[b2_row : b2_row + 8, :]
-
     x_sends = []
     for k in (2, 1):
         cp = copy(xall.at[q], xall.at[q], s_x.at[k], r_x.at[q], z * PLANE + mates[k])
@@ -319,13 +319,9 @@
 
     for k in range(1, PLANE):
         copy(dsend, drecv.at[mates[k]], s_d.at[0], r_d.at[mates[k]], me).wait_recv()
-    dw2 = jnp.zeros((16, quarter), F32)
     for p in range(PLANE):
         h = hid[p]
-        d = halves(drecv[p])
-        dw2 = dw2 + dot3(d, halves(h), NN)
-        hid[p] = dot3(d, w2h, TN) * (1.0 - h * h)
-    dp = [halves(hid[p]) for p in range(PLANE)]
+        dh[p], dlow[p] = halves(dot3(halves(drecv[p]), w2h, TN) * (1.0 - h * h))
 
     def hop(d, p, right, act):
         side = 0 if right else 1
@@ -342,7 +338,7 @@
         cols = pl.ds(pl.multiple_of(d * chunk, chunk), chunk)
         g = jnp.zeros((chunk, quarter), F32)
         for p in range(PLANE):
-            g = g + dot3((xh[p, :, cols], xl[p, :, cols]), dp[p], TN)
+            g = g + dot3((xh[p, :, cols], xl[p, :, cols]), (dh[p], dlow[p]), TN)
         dwz[d] = g
 
         @pl.when((z == 0) & (d > 0))
@@ -361,6 +357,9 @@
         copy(dwz.at[0, piece], zrecv.at[side, d, piece], s_z.at[0, 0], r_z.at[side, d, p], me).wait_recv()
         dwz[d, piece, :] = dwz[d, piece, :] + zrecv[side, d, piece, :]
 
+    dw2 = jnp.zeros((16, quarter), F32)
+    for p in range(PLANE):
+        dw2 = dw2 + dot3(halves(drecv[p]), halves(hid[p]), NN)
     acc = jnp.zeros((16 * blocks, LANES), F32)
     for o in range(OUT):
         spot, mask = select(o)
@@ -391,18 +390,16 @@
     def _():
         w2recv[last] = w2send[...]
 
-    for dr in range(DEPTH - 1, 0, -1):
-        dl_ = DEPTH - 1 - dr
-        for p in range(PLANE):
-            @pl.when((z > 0) & (z < dr))
-            def _(p=p):
-                add_arrived(dr, p, True)
-                hop(dr, p, True, "start")
-
-            @pl.when((z < DEPTH - 1) & (z > dl_))
-            def _(p=p):
-                add_arrived(dl_, p, False)
-                hop(dl_, p, False, "start")
+    for at, right, end, mid in ((1, True, 3, 2), (2, False, 0, 1)):
+        @pl.when(z == at)
+        def _(right=right, end=end, mid=mid):
+            for p in range(PLANE):
+                add_arrived(end, p, right)
+                hop(end, p, right, "start")
+            for p in range(PLANE):
+                for d, way in ((3 - end, not right), (mid, right)):
+                    add_arrived(d, p, way)
+                    hop(d, p, way, "start")
 
     for p in range(PLANE):
         @pl.when(z > 0)
@@ -485,6 +482,18 @@
     @pl.when(me < last)
     def _():
         copy(w2send, w2recv.at[me], s_g, r_g.at[me], last).wait_send()
+
+
+def update(scale_data, grad, par, mom, noi, par_out, mom_out):
+    position = (lax.axis_index("dp") * par.shape[0] + iota(par.shape, 0)) * LANES
+    force = scale_data * grad[...] + prior_precision(position) * par[...]
+    m = (
+        (1.0 - step_size * friction) * mom[...]
+        - step_size * force
+        + math.sqrt(2.0 * friction * step_size) * noi[...]
+    )
+    mom_out[...] = m
+    par_out[...] = par[...] + step_size * m
 
 
 def fused_body(params, momentum, noise_draws, images, labels, indices):
@@ -506,7 +515,8 @@
     scratch = [
         vm(PLANE, pad, quarter), vm(wide, quarter), vm(PLANE, batch, wide),
         pltpu.VMEM((PLANE, batch, wide), BF), pltpu.VMEM((PLANE, batch, wide), BF),
-        vm(PLANE, batch, quarter), vm(PLANE, per, LANES), vm(per, LANES), vm(8, LANES),
+        vm(PLANE, batch, quarter),
+        pltpu.VMEM((PLANE, batch, quarter), BF), pltpu.VMEM((PLANE, batch, quarter), BF), vm(PLANE, per, LANES), vm(per, LANES), vm(8, LANES),
         vm(16 * blocks, LANES), vm(16, quarter),
         vm(PLANE, 16, batch), vm(PLANE, 16, batch), vm(16, batch), vm(PLANE, 16, batch),
         vm(DEPTH, chunk, quarter), vm(2, DEPTH, chunk, quarter),
@@ -534,15 +544,13 @@
         labels.reshape(1, -1),
         indices,
     )
-    position = lax.axis_index("dp") * shard + iota(flat, 0) * LANES
-    params = params.reshape(flat)
-    force = images.shape[0] / batch * grad + prior_precision(position) * params
-    momentum = (
-        (1.0 - step_size * friction) * momentum.reshape(flat)
-        - step_size * force
-        + math.sqrt(2.0 * friction * step_size) * noise_draws.reshape(flat)
-    )
-    return ((params + step_size * momentum).reshape(-1), momentum.reshape(-1), loss)
+    p, m = pl.pallas_call(
+        functools.partial(update, images.shape[0] / batch),
+        out_shape=(jax.ShapeDtypeStruct(flat, F32),) * 2,
+        in_specs=[vmem] * 4,
+        out_specs=(vmem, vmem),
+    )(grad, params.reshape(flat), momentum.reshape(flat), noise_draws.reshape(flat))
+    return (p.reshape(-1), m.reshape(-1), loss)
 
 
 def solution(mesh):

time: 86.2 us -> 66.7 us (0.77)
  Pallas kernels: 79.7 us -> 64.1 us
  other arithmetic: 3.18 us -> 0 us
    pallas_call x1, Pallas kernels: 79.7 us -> 61.9 us  [fused_body(): pl.pallas_call(functools.partial(kernel, dims), out_shape=(jax.ShapeDtype...]
    pallas_call x0 -> x1, Pallas kernels: none -> 2.21 us  [fused_body(): pl.pallas_call(functools.partial(update, images.shape[0] / batch), out_sh...]
    reshape x1 -> x0, other arithmetic: 1.97 us -> none  [fused_body(): (params + step_size * momentum).reshape(-1)]
    mul x1 -> x0, other arithmetic: 1.19 us -> none  [fused_body(): math.sqrt(2.0 * friction * step_size) * noise_draws.reshape(flat)]
where the time goes in v3:
time: 66.7 us; the launch traced here: 66.5 us
  Pallas kernels  64.1 us (96%)
  between operations  2.4 us (4%)
    pallas_call x1, Pallas kernels, fused_body(): pl.pallas_call(functools.partial(kernel, dims), out_shape=(jax.ShapeDtype...  61.9 us
    pallas_call x1, Pallas kernels, fused_body(): pl.pallas_call(functools.partial(update, images.shape[0] / batch), out_sh...  2.21 us

profile of v3, /device:TPU:0, one launch (start us, length us, event | category | flops | bytes accessed | tf_op | source)
XLA Modules:
  0.0 66.5 jit_solution(4360616522130866630)
XLA Ops:
  0.6 61.9 %shard_map.85 = (f32[464,128]{1,0:T(8,128)}, f32[1]{0:T(128)}) custom-call(f32[464,128]{1,0:T(8,128)} %bitcast.7, f32[448,512]{1,0:T(8,128)} %bitcast.9, s32[1,512]{1,0:T(1,128)} %bitcast.12, s32[1,256]{1,0:T(1,128)} %idx.1), custom_call_target="tpu_custom_call" | custom-call | tf_op jit(solution)/shard_map/pallas_call | solution.py:529
  62.5 2.2 %shard_map.86 = (f32[464,128]{1,0:T(8,128)}, f32[464,128]{1,0:T(8,128)}) custom-call(f32[464,128]{1,0:T(8,128)} %get-tuple-element.7.grad, f32[464,128]{1,0:T(8,128)} %bitcast.8, f32[464,128]{1,0:T(8,128)} %bitcast.10, f32[464,128]{1,0:T(8,128)} %bitcast.11), custom_call_target="tpu_custom_call" | custom-call | tf_op jit(solution)/shard_map/pallas_call | solution.py:547

commit v4 on v3

--- a/solution.py
+++ b/solution.py
@@ -180,6 +180,18 @@
         w2buf[...] = w2src[PLANE - 1]
         b2buf[...] = par[b2_row : b2_row + 8, :]
 
+    def w_arrived(s):
+        copy(wsend.at[0], wpiece(s), s_wp.at[0], r_w.at[s], me).wait_recv()
+
+    def x_arrived(k):
+        copy(xall.at[q], xall.at[mates[k]], s_x.at[0], r_x.at[mates[k]], me).wait_recv()
+
+    def pass_on(k):
+        s = z * PLANE + mates[k]
+        w_arrived(s)
+        zsend(wpiece(s), s, (0, 1), "start")
+
+    pass_on(1)
     pool = img.shape[1]
     onehot = (iota((pool, batch), 0) == idx[...]).astype(BF)
     target = dot(jnp.broadcast_to(lab[...], (8, pool)).astype(BF), onehot, NN)[0:1, :]
@@ -197,16 +209,8 @@
         cp.start()
         x_sends.append(cp)
 
-    def w_arrived(s):
-        copy(wsend.at[0], wpiece(s), s_wp.at[0], r_w.at[s], me).wait_recv()
-
-    def x_arrived(k):
-        copy(xall.at[q], xall.at[mates[k]], s_x.at[0], r_x.at[mates[k]], me).wait_recv()
-
-    for k in (1, 2, 3):
-        s = z * PLANE + mates[k]
-        w_arrived(s)
-        zsend(wpiece(s), s, (0, 1), "start")
+    pass_on(2)
+    pass_on(3)
 
     def far(t, fn):
         for sign, d in ((-1, 0), (1, 1)):
@@ -226,17 +230,19 @@
 
     def product(zs, first=False):
         at = pl.ds(pl.multiple_of(zs * chunk, chunk), chunk)
-        w = halves(wbuf[at, :])
+        w, w_low = halves(wbuf[at, :])
+        both = jnp.concatenate([w, w], axis=0)
         for p in range(PLANE):
-            part = dot3((xh[p, :, at], xl[p, :, at]), w, NN)
+            high = xh[p, :, at]
+            part = dot(jnp.concatenate([high, xl[p, :, at]], axis=1), both, NN) + dot(high, w_low, NN)
             hid[p] = part if first else hid[p] + part
 
     far(1, forward)
+    far(2, forward)
     x_arrived(2)
     cp = copy(xall.at[mates[2]], xall.at[mates[2]], s_x.at[3], r_x.at[mates[2]], z * PLANE + mates[1])
     cp.start()
     x_sends.append(cp)
-    far(2, forward)
 
     @pl.when(me < last)
     def _():
@@ -263,6 +269,8 @@
                 jnp.where(mask, r[16 * j : 16 * (j + 1), :], 0.0), axis=0, keepdims=True
             )
     w2h = halves(w2t[...])
+    w2_rows = jnp.concatenate(w2h, axis=0)
+    w2_deep = jnp.concatenate([w2h[0], w2h[1], w2h[0]], axis=0)
     x_arrived(1)
     x_arrived(3)
     for p in range(PLANE):
@@ -279,7 +287,9 @@
         o = mates[k]
         h = jnp.tanh(hid[o])
         hid[o] = h
-        part = dot3(w2h, halves(h), NT)
+        h, low = halves(h)
+        part = dot(w2_rows, h, NT)
+        part = part[0:16] + (part[16:32] + dot(w2h[0], low, NT))
         if k == 0:
             mine = part
         else:
@@ -321,7 +331,9 @@
         copy(dsend, drecv.at[mates[k]], s_d.at[0], r_d.at[mates[k]], me).wait_recv()
     for p in range(PLANE):
         h = hid[p]
-        dh[p], dlow[p] = halves(dot3(halves(drecv[p]), w2h, TN) * (1.0 - h * h))
+        d, d_low = halves(drecv[p])
+        back = dot(jnp.concatenate([d, d, d_low], axis=0), w2_deep, TN)
+        dh[p], dlow[p] = halves(back * (1.0 - h * h))
 
     def hop(d, p, right, act):
         side = 0 if right else 1

time: 66.7 us -> 64.3 us (0.964)
  the two profiles are of different devices: /device:TPU:0 before, /device:TPU:11 now
where the time goes in v4:
time: 64.3 us; the launch traced here: 64.1 us
  Pallas kernels  61.7 us (96%)
  between operations  2.4 us (4%)
    pallas_call x1, Pallas kernels, fused_body(): pl.pallas_call(functools.partial(kernel, dims), out_shape=(jax.ShapeDtype...  59.5 us
    pallas_call x1, Pallas kernels, fused_body(): pl.pallas_call(functools.partial(update, images.shape[0] / batch), out_sh...  2.21 us

profile of v4, /device:TPU:11, one launch (start us, length us, event | category | flops | bytes accessed | tf_op | source)
XLA Modules:
  0.0 64.1 jit_solution(1510782882324465018)
XLA Ops:
  0.6 59.5 %shard_map.85 = (f32[464,128]{1,0:T(8,128)}, f32[1]{0:T(128)}) custom-call(f32[464,128]{1,0:T(8,128)} %bitcast.7, f32[448,512]{1,0:T(8,128)} %bitcast.9, s32[1,512]{1,0:T(1,128)} %bitcast.12, s32[1,256]{1,0:T(1,128)} %idx.1), custom_call_target="tpu_custom_call" | custom-call | tf_op jit(solution)/shard_map/pallas_call | solution.py:541
  60.1 2.2 %shard_map.86 = (f32[464,128]{1,0:T(8,128)}, f32[464,128]{1,0:T(8,128)}) custom-call(f32[464,128]{1,0:T(8,128)} %get-tuple-element.7.grad, f32[464,128]{1,0:T(8,128)} %bitcast.8, f32[464,128]{1,0:T(8,128)} %bitcast.10, f32[464,128]{1,0:T(8,128)} %bitcast.11), custom_call_target="tpu_custom_call" | custom-call | tf_op jit(solution)/shard_map/pallas_call | solution.py:559
